TPU v7x, 32 devices: a whole 2x2x4 slice. The times are simulated.
32 devices in a mesh: ty: 4 (over x, core), tx: 8 (over z, y).
Axes of the slice: x: 2, y: 2, z: 4, core: 2. Of those that a mesh axis runs over, the one named last changes fastest.
Arguments:
- exposures: float32 [256, 128, 128], P(('ty', 'tx')), may hold values from -70 to 70
- point_spread: float32 [256, 31, 31], P(('ty', 'tx')), may hold values from 0.0001 to 1
- warp_steps: int32 [256, 2], P(('ty', 'tx')), may hold values from 0 to 3
- column: int32 [256, 1], P(('ty', 'tx')), may hold values from 0 to 7; in each aligned block of 8 rows (0 to 7, 8 to 15, ...) at most 2 rows name the same one
- block_cell: int32 [256], P(('ty', 'tx')), may hold values from 0 to 15
Outputs:
- solution: float32 [2048, 4096], P('ty', 'tx')
- residual: float32 [2048, 4096], P('ty', 'tx')
Inputs may be any that keep to these rules, and one draw needn't show every extreme that they name: `column`: among the 8 frame blocks of one device (aligned blocks of 8 rows) no value occurs more than 2 times, and in some such block one value occurs exactly 2 times.
All inputs are finite; a program needn't handle non-finite values.
Results may differ from a plain program's by a relative error of at most 0.0042.
Values may be sent and summed in bfloat16 or wider, within the bound.
A program may use at most 192 MiB of HBM per device.

v0:
```python
import functools

import jax
import jax.numpy as jnp
from jax import lax
from jax.experimental import pallas as pl
from jax.experimental.pallas import tpu as pltpu
from jax.sharding import PartitionSpec as P

TILE = 512
SUB = 4
ITERS = 2
GROUP = 32
LANES = 128

damping = 0.05


def make_kernels(point_spread, warp_steps):
    tap_count = point_spread.shape[-1] + 1
    totals = jnp.sum(point_spread, axis=(1, 2), keepdims=True)
    padded = jnp.pad(point_spread / totals, ((0, 0), (0, 1), (0, 1)))
    row_frac = (warp_steps[:, 0].astype(jnp.float32) / SUB)[:, None, None]
    col_frac = (warp_steps[:, 1].astype(jnp.float32) / SUB)[:, None, None]
    shifted = jnp.pad(padded, ((0, 0), (0, 0), (1, 0)))[:, :, :tap_count]
    blended = (1.0 - col_frac) * padded + col_frac * shifted
    lowered = jnp.pad(blended, ((0, 0), (1, 0), (0, 0)))[:, :tap_count, :]
    return ((1.0 - row_frac) * blended + row_frac * lowered).astype(jnp.bfloat16)


def turn(value, shift, axis):
    size = value.shape[axis]
    shift = shift % size
    return value if shift == 0 else pltpu.roll(value, shift, axis)


def lane_group(shape, width):
    return lax.broadcasted_iota(jnp.int32, shape, 1) // width


def pick_groups(groups, parts):
    value = parts[-1]
    for number in range(len(parts) - 2, -1, -1):
        value = jnp.where(groups == number, parts[number], value)
    return value


def toeplitz(rows):
    tiles = []
    for j in range(8):
        halves = []
        for half in range(2):
            spread = jnp.broadcast_to(rows[2 * j + half : 2 * j + half + 1], (GROUP, LANES))
            halves.append(pltpu.roll(spread, 0, 1, stride=1, stride_axis=0))
        tiles.append(jnp.concatenate(halves, axis=1))
    return jnp.concatenate(tiles, axis=0).astype(jnp.bfloat16)


def blur(left, right, matrix):
    groups = lane_group(left.shape, GROUP)
    low = groups < 2
    by32, by64, by96 = turn(left, 32, 1), turn(left, 64, 1), turn(left, 96, 1)
    end32, end96 = turn(right, 32, 1), turn(right, 96, 1)
    framed = [
        jnp.where(low, left, by64),
        jnp.where(low, by96, by32),
        jnp.where(low, by64, left),
        pick_groups(groups, [by32, end32, by96, end96]),
    ]
    summed = []
    for part in framed:
        first = jnp.where(low, part, turn(part, -1, 0))
        stacked = jnp.concatenate([first, turn(first, -2, 0)], axis=1).astype(jnp.bfloat16)
        product = lax.dot_general(
            stacked, matrix, (((1,), (1,)), ((), ())), preferred_element_type=jnp.float32
        )
        joined = product[:, :LANES] + turn(product[:, LANES:], -16, 0)
        summed.append(pick_groups(groups, [turn(joined, -4 * j, 0) for j in range(4)]))
    total = pick_groups(groups, summed)
    for step in range(1, 4):
        chosen = pick_groups(groups, [summed[(j + step) % 4] for j in range(4)])
        total = total + turn(chosen, 32 * step, 1)
    return total


def blur_back(image, matrix):
    groups = lane_group(image.shape, GROUP)
    low = groups < 2
    turned = [turn(image, 32 * step, 1) for step in range(4)]
    folded = []
    for h in range(4):
        spread = pick_groups(groups, [turned[(j - h) % 4] for j in range(4)])
        first = pick_groups(groups, [turn(spread, 4 * j, 0) for j in range(4)])
        stacked = jnp.concatenate([first, turn(first, 16, 0)], axis=1).astype(jnp.bfloat16)
        product = jnp.dot(stacked, matrix, preferred_element_type=jnp.float32)
        joined = product[:, :LANES] + turn(product[:, LANES:], 2, 0)
        shifted = jnp.where(low, joined, turn(joined, 1, 0))
        folded.append(shifted + turn(shifted, 64, 1))
    one, three = turn(folded[1], 32, 1), turn(folded[3], 32, 1)
    zero = jnp.zeros_like(one)
    left = jnp.where(low, folded[0], folded[2]) + pick_groups(groups, [zero, one, one, three])
    right = jnp.where(groups == 0, three, 0.0)
    return left, right


def place(total_ref, cell, per_row, block, patch):
    left, right = patch
    rows = pl.ds(pl.multiple_of(cell // per_row * block, block), left.shape[0])
    start = pl.multiple_of(cell % per_row * block, block)
    total_ref[rows, pl.ds(start, block)] += left
    total_ref[rows, pl.ds(pl.multiple_of(start + block, block), block)] += right


def pack_kernel(count, source_ref, tag_ref, exposures_ref, taps_ref, out_ref):
    block = exposures_ref.shape[1]

    @pl.loop(0, count)
    def _(slot):
        origin = source_ref[slot]
        out_ref[slot, :block, :] = exposures_ref[origin].astype(jnp.bfloat16)
        out_ref[slot, block : block + 16, :] = taps_ref[origin]
        out_ref[slot, block + 16 :, :] = jnp.full((16, LANES), tag_ref[slot], jnp.float32).astype(
            jnp.bfloat16
        )


def first_kernel(count, per_row, block, cell_ref, frames_ref, total_ref, matrix_ref):
    total_ref[...] = jnp.zeros_like(total_ref)

    @pl.loop(0, count)
    def _(slot):
        cell = cell_ref[slot]

        @pl.when(cell >= 0)
        def _():
            frame = frames_ref[slot]
            matrix = toeplitz(frame[block : block + 16].astype(jnp.float32))
            matrix_ref[slot] = matrix
            image = frame[:block].astype(jnp.float32)
            image = jnp.concatenate([image, jnp.zeros((GROUP, LANES), jnp.float32)], axis=0)
            place(total_ref, cell, per_row, block, blur_back(image, matrix))


def normal_kernel(count, per_row, block, cell_ref, field_ref, matrix_ref, total_ref):
    total_ref[...] = jnp.zeros_like(total_ref)
    window = block + GROUP

    @pl.loop(0, count)
    def _(slot):
        cell = cell_ref[slot]

        @pl.when(cell >= 0)
        def _():
            matrix = matrix_ref[slot]
            rows = pl.ds(pl.multiple_of(cell // per_row * block, block), window)
            start = pl.multiple_of(cell % per_row * block, block)
            left = field_ref[rows, pl.ds(start, block)].astype(jnp.float32)
            right = field_ref[rows, pl.ds(pl.multiple_of(start + block, block), block)].astype(
                jnp.float32
            )
            modelled = blur(left, right, matrix).astype(jnp.bfloat16).astype(jnp.float32)
            inside = lax.broadcasted_iota(jnp.int32, modelled.shape, 0) < block
            image = jnp.where(inside, modelled, 0.0)
            place(total_ref, cell, per_row, block, blur_back(image, matrix))


def sum_kernel(axes, own_ref, out_ref, *scratch):
    barrier = pltpu.get_barrier_semaphore()
    peers = 0
    for axis, size in axes:
        me = lax.axis_index(axis)
        for step in range(1, size):
            pl.semaphore_signal(
                barrier,
                inc=1,
                device_id={axis: lax.rem(me + step, size)},
                device_id_type=pl.DeviceIdType.MESH,
            )
        peers += size - 1
    pl.semaphore_wait(barrier, peers)
    source = own_ref
    for number, (axis, size) in enumerate(axes):
        total_ref, landed, sent, received = scratch[4 * number : 4 * number + 4]
        me = lax.axis_index(axis)
        copies = [
            pltpu.make_async_remote_copy(
                src_ref=source,
                dst_ref=landed.at[step - 1],
                send_sem=sent.at[step - 1],
                recv_sem=received.at[step - 1],
                device_id={axis: lax.rem(me + step, size)},
                device_id_type=pl.DeviceIdType.MESH,
            )
            for step in range(1, size)
        ]
        for copy in copies:
            copy.start()
        for copy in copies:
            copy.wait()
        total = source[...]
        for step in range(size - 1):
            total = total + landed[step]
        total_ref[...] = total
        source = total_ref
    out_ref[...] = source[...]


def sum_over_mesh(values, number):
    axes = [(axis, lax.axis_size(axis)) for axis in ("ty", "tx")]
    shape = (8, LANES)
    scratch = []
    for _, size in axes:
        scratch += [
            pltpu.VMEM(shape, jnp.float32),
            pltpu.VMEM((size - 1,) + shape, jnp.float32),
            pltpu.SemaphoreType.DMA((size - 1,)),
            pltpu.SemaphoreType.DMA((size - 1,)),
        ]
    rows = jnp.pad(values, (0, shape[0] - values.shape[0]))
    summed = pl.pallas_call(
        functools.partial(sum_kernel, axes),
        out_shape=jax.ShapeDtypeStruct(shape, jnp.float32),
        in_specs=[vmem()],
        out_specs=vmem(),
        scratch_shapes=scratch,
        compiler_params=pltpu.CompilerParams(collective_id=number, has_side_effects=True),
        name="sum_mesh",
    )(jnp.broadcast_to(rows[:, None], shape))
    return [summed[row, 0] for row in range(values.shape[0])]


def vmem():
    return pl.BlockSpec(memory_space=pltpu.VMEM)


def smem():
    return pl.BlockSpec(memory_space=pltpu.SMEM)


def flat_strip(strip):
    count = LANES // strip.shape[1]
    parts = strip.reshape(count, strip.shape[0] // count, strip.shape[1])
    return jnp.concatenate([parts[i] for i in range(count)], axis=1)


def tall_strip(flat, shape):
    count = LANES // shape[1]
    return jnp.concatenate([flat[:, i * shape[1] : (i + 1) * shape[1]] for i in range(count)], axis=0)


def share_edges(value, axis, dim, width):
    size, length = lax.axis_size(axis), value.shape[dim]
    position = lax.axis_index(axis)
    up = [(i, i + 1) for i in range(size - 1)]
    down = [(j, i) for i, j in up]
    first = lax.slice_in_dim(value, 0, 2 * width, axis=dim)
    middle = lax.slice_in_dim(value, 2 * width, length - 2 * width, axis=dim)
    last = lax.slice_in_dim(value, length - 2 * width, length, axis=dim)
    if dim == 1:
        before = lax.ppermute(flat_strip(last), axis, up)
        after = lax.ppermute(flat_strip(first), axis, down)
        before, after = tall_strip(before, last.shape), tall_strip(after, first.shape)
    else:
        before = lax.ppermute(last, axis, up)
        after = lax.ppermute(first, axis, down)
    index = lax.broadcasted_iota(jnp.int32, first.shape, dim)
    first = jnp.where((position > 0) | (index >= width), first + before, 0.0)
    last = jnp.where((position < size - 1) | (index < width), last + after, 0.0)
    return jnp.concatenate([first, middle, last], axis=dim)


def body(exposures, point_spread, warp_steps, column, block_cell):
    frame_count, block = exposures.shape[:2]
    tap_count = point_spread.shape[1] + 1
    margin = tap_count // 2
    tx_size = lax.axis_size("tx")
    capacity = max(2, 2 * frame_count // tx_size)
    slot_count = tx_size * capacity
    per_row = TILE // block
    extent = TILE + 2 * margin
    wide = TILE + block
    taps = make_kernels(point_spread, warp_steps)
    taps = jnp.pad(taps, ((0, 0), (0, 0), (0, 64 - tap_count))).reshape(frame_count, 16, LANES)

    target = column[:, 0]
    earlier = jnp.arange(frame_count)[:, None] > jnp.arange(frame_count)[None, :]
    matching = target[:, None] == target[None, :]
    standing = jnp.sum(jnp.where(earlier & matching, 1, 0), axis=1)
    slot_index = target * capacity + standing
    chosen = slot_index[None, :] == jnp.arange(slot_count)[:, None]
    source = jnp.sum(jnp.where(chosen, jnp.arange(frame_count)[None, :], 0), axis=1).astype(jnp.int32)
    tag = jnp.sum(jnp.where(chosen, block_cell[None, :] + 1, 0), axis=1).astype(jnp.float32)

    packed = pl.pallas_call(
        functools.partial(pack_kernel, slot_count),
        out_shape=jax.ShapeDtypeStruct((slot_count, block + 32, LANES), jnp.bfloat16),
        in_specs=[smem(), smem(), vmem(), vmem()],
        out_specs=vmem(),
        name="pack",
    )(source, tag, exposures, taps)
    frames = lax.all_to_all(packed, "tx", split_axis=0, concat_axis=0, tiled=True)
    cells = frames[:, block + 16, 0].astype(jnp.int32) - 1

    total, matrices = pl.pallas_call(
        functools.partial(first_kernel, slot_count, per_row, block),
        out_shape=(
            jax.ShapeDtypeStruct((extent, wide), jnp.float32),
            jax.ShapeDtypeStruct((slot_count, 256, 256), jnp.bfloat16),
        ),
        in_specs=[smem(), vmem()],
        out_specs=(vmem(), vmem()),
        name="first_adjoint",
    )(cells, frames)

    def finish(total):
        value = share_edges(total[:, :extent], "ty", 0, margin)
        return share_edges(value, "tx", 1, margin)

    def inner(value):
        return value[margin : margin + TILE, margin : margin + TILE]

    def products(pairs):
        return tuple(jnp.sum(inner(left * right)) for left, right in pairs)

    residual = finish(total)
    direction = residual
    solution = jnp.zeros((TILE, TILE), jnp.float32)
    norm_now = None
    for iteration in range(ITERS):
        field = jnp.pad(direction.astype(jnp.bfloat16), ((0, 0), (0, wide - extent)))
        total = pl.pallas_call(
            functools.partial(normal_kernel, slot_count, per_row, block),
            out_shape=jax.ShapeDtypeStruct((extent, wide), jnp.float32),
            in_specs=[smem(), vmem(), vmem()],
            out_specs=vmem(),
            name="normal",
        )(cells, field, matrices)
        applied = finish(total) + damping * direction
        last = iteration + 1 == ITERS
        pairs = [(direction, applied)]
        if not last:
            pairs = pairs + [(residual, applied), (applied, applied)]
        if norm_now is None:
            pairs = pairs + [(residual, residual)]
        sums = sum_over_mesh(jnp.stack(products(pairs)), iteration)
        if norm_now is None:
            norm_now = sums[-1]
        step_size = norm_now / sums[0]
        solution = solution + step_size * inner(direction)
        residual = residual - step_size * applied
        if not last:
            norm_next = norm_now - 2.0 * step_size * sums[1] + step_size * step_size * sums[2]
            direction = residual + norm_next / norm_now * direction
            norm_now = norm_next
    return solution, inner(residual)


def solution(mesh):
    placed = (
        P(("ty", "tx"), None, None),
        P(("ty", "tx"), None, None),
        P(("ty", "tx"), None),
        P(("ty", "tx"), None),
        P(("ty", "tx")),
    )
    return jax.shard_map(
        body, mesh=mesh, in_specs=placed, out_specs=(P("ty", "tx"), P("ty", "tx")), check_vma=False
    )
```

profile of v0, /device:TPU:0, one launch (start us, length us, event | category | flops | bytes accessed | tf_op | source)
XLA Modules:
  0.0 186.5 jit_solution(1358936172419815074)
XLA Ops:
  8.0 2.0 %pack.1 = bf16[16,160,128]{2,1,0:T(8,128)(2,1)} custom-call(s32[16]{0:T(128)} %get-tuple-element.10.source_ref, f32[16]{0:T(128)} %convert_element_type.53.tag_ref, f32[8,128,128]{2,1,0:T(8,128)} %exposures_ref.1, bf16[8,16,128]{2,1,0:T(8,128)(2,1)} %reshape.106.taps_ref), custom_call_target="tpu_custom_call" | custom-call | tf_op jit(solution)/shard_map/pack/pallas_call | solution.py:294
  10.0 7.3 %all-to-all-start = ((bf16[16,160,128]{2,1,0:T(8,128)(2,1)}), bf16[16,160,128]{2,1,0:T(8,128)(2,1)S(1)}, u32[]{:S(2)}, u32[]{:S(2)}) async-start(bf16[16,160,128]{2,1,0:T(8,128)(2,1)} %pack.1), calls=%async_computation | async-start | bytes 1310720 | tf_op jit(solution)/shard_map/all_to_all | solution.py:301
  17.3 17.3 %all-to-all-done.frames_ref = bf16[16,160,128]{2,1,0:T(8,128)(2,1)S(1)} async-done(((bf16[16,160,128]{2,1,0:T(8,128)(2,1)}), bf16[16,160,128]{2,1,0:T(8,128)(2,1)S(1)}, u32[]{:S(2)}, u32[]{:S(2)}) %all-to-all-start) | async-done | bytes 655392 | tf_op jit(solution)/shard_map/all_to_all | solution.py:301
  35.5 5.2 %first_adjoint.1 = (f32[544,640]{1,0:T(8,128)}, bf16[16,256,256]{2,1,0:T(8,128)(2,1)}) custom-call(s32[16]{0:T(128)} %fusion.28.cell_ref, bf16[16,160,128]{2,1,0:T(8,128)(2,1)} %copy-done.4), custom_call_target="tpu_custom_call" | custom-call | tf_op jit(solution)/shard_map/first_adjoint/pallas_call | solution.py:304
  41.6 1.8 collective-permute-start
  43.4 1.3 collective-permute-start.1
  45.8 1.4 slice.353
  47.1 2.7 %collective-permute-done.1 = f32[32,544]{1,0:T(8,128)S(1)} collective-permute-done((f32[32,544]{1,0:T(8,128)S(1)}, f32[32,544]{1,0:T(8,128)S(1)}, u32[]{:S(2)}, u32[]{:S(2)}) %collective-permute-start.1) | collective-permute-done | bytes 69664 | tf_op jit(solution)/shard_map/ppermute | solution.py:265
  51.0 1.3 collective-permute-start.3
  52.4 8.0 %collective-permute-start.2 = (f32[136,128]{1,0:T(8,128)S(1)}, f32[136,128]{1,0:T(8,128)S(1)}, u32[]{:S(2)}, u32[]{:S(2)}) collective-permute-start(f32[136,128]{1,0:T(8,128)S(1)} %get-tuple-element.42), channel_id=1, source_target_pairs={{0,1},{1,2},{2,3},{3,4},{4,5},{5,6},{6,7},{8,9},{9,10},{10,11},{11... | collective-permute-start | bytes 208904 | tf_op jit(solution)/shard_map/ppermute | solution.py:260
  61.0 1.4 collective-permute-done.2
  64.0 6.7 %normal.2 = f32[544,640]{1,0:T(8,128)} custom-call(s32[16]{0:T(128)} %fusion.28.cell_ref, bf16[544,640]{1,0:T(8,128)(2,1)} %pad.35.field_ref, bf16[16,256,256]{2,1,0:T(8,128)(2,1)} %get-tuple-element.5.matrix_ref), custom_call_target="tpu_custom_call" | custom-call | tf_op jit(solution)/shard_map/normal/pallas_call | solution.py:331
  71.6 6.7 %collective-permute-start.4 = (f32[32,544]{1,0:T(8,128)S(1)}, f32[32,544]{1,0:T(8,128)S(1)}, u32[]{:S(2)}, u32[]{:S(2)}) collective-permute-start(f32[32,544]{1,0:T(8,128)S(1)} %get-tuple-element.38), channel_id=1, source_target_pairs={{0,8},{8,16},{16,24},{1,9},{9,17},{17,25},{2,10},{10,18},{18,26},{... | collective-permute-start | bytes 208904 | tf_op jit(solution)/shard_map/ppermute | solution.py:264
  78.3 1.3 collective-permute-start.5
  80.6 1.4 slice.441
  84.2 1.3 collective-permute-start.7
  85.6 12.3 %collective-permute-start.6 = (f32[136,128]{1,0:T(8,128)S(1)}, f32[136,128]{1,0:T(8,128)S(1)}, u32[]{:S(2)}, u32[]{:S(2)}) collective-permute-start(f32[136,128]{1,0:T(8,128)S(1)} %get-tuple-element.30), channel_id=1, source_target_pairs={{0,1},{1,2},{2,3},{3,4},{4,5},{5,6},{6,7},{8,9},{9,10},{10,11},{11... | collective-permute-start | bytes 208904 | tf_op jit(solution)/shard_map/ppermute | solution.py:260
  98.5 1.4 collective-permute-done.6
  101.7 1.3 multiply_reduce_fusion.3
  103.0 2.0 %select_maximum_fusion.6 = f32[8]{0:T(128)S(1)} fusion(f32[1]{0:T(128)} %bitcast.5, f32[1]{0:T(128)} %bitcast.4, f32[1]{0:T(128)} %bitcast.3), kind=kLoop, calls=%fused_computation.83 | loop fusion | flops 64 | bytes 44 | tf_op jit(solution)/shard_map/stack | solution.py:345
  105.7 15.9 %sum_mesh.2 = f32[8,128]{1,0:T(8,128)} custom-call(f32[8,128]{1,0:T(8,128)} %broadcast_in_dim.72.own_ref), custom_call_target="tpu_custom_call" | custom-call | tf_op jit(solution)/shard_map/sum_mesh/pallas_call | solution.py:220
  121.6 1.4 fusion.44
  126.9 2.7 %fusion.30 = (bf16[544,544]{1,0:T(8,128)(2,1)S(1)}, f32[544,544]{1,0:T(8,128)S(1)}, f32[544,544]{1,0:T(8,128)}) fusion(f32[544,544]{1,0:T(8,128)S(1)} %get-tuple-element.15, f32[]{:T(128)S(6)} %div.34, f32[544,544]{1,0:T(8,128)} %copy-done, f32[]{:T(128)S(6)} %div.33), kind=kLoop, calls=%fused_computation.93 | loop fusion | flops 1479680 | bytes 5326856 | tf_op jit(solution)/shard_map/convert_element_type | solution.py:330
  130.5 6.7 %normal.3 = f32[544,640]{1,0:T(8,128)} custom-call(s32[16]{0:T(128)} %fusion.28.cell_ref, bf16[544,640]{1,0:T(8,128)(2,1)} %pad.37.field_ref, bf16[16,256,256]{2,1,0:T(8,128)(2,1)} %get-tuple-element.5.matrix_ref), custom_call_target="tpu_custom_call" | custom-call | tf_op jit(solution)/shard_map/normal/pallas_call | solution.py:331
  138.2 3.7 %collective-permute-start.8 = (f32[32,544]{1,0:T(8,128)S(1)}, f32[32,544]{1,0:T(8,128)S(1)}, u32[]{:S(2)}, u32[]{:S(2)}) collective-permute-start(f32[32,544]{1,0:T(8,128)S(1)} %get-tuple-element.26), channel_id=1, source_target_pairs={{0,8},{8,16},{16,24},{1,9},{9,17},{17,25},{2,10},{10,18},{18,26},{... | collective-permute-start | bytes 208904 | tf_op jit(solution)/shard_map/ppermute | solution.py:264
  141.9 1.3 collective-permute-start.9
  144.2 1.4 slice.462
  148.7 10.6 %collective-permute-start.10 = (f32[136,128]{1,0:T(8,128)S(1)}, f32[136,128]{1,0:T(8,128)S(1)}, u32[]{:S(2)}, u32[]{:S(2)}) collective-permute-start(f32[136,128]{1,0:T(8,128)S(1)} %get-tuple-element.18), channel_id=1, source_target_pairs={{0,1},{1,2},{2,3},{3,4},{4,5},{5,6},{6,7},{8,9},{9,10},{10,11},{11... | collective-permute-start | bytes 208904 | tf_op jit(solution)/shard_map/ppermute | solution.py:260
  159.7 1.4 collective-permute-done.10
  165.5 15.4 %sum_mesh.3 = f32[8,128]{1,0:T(8,128)} custom-call(f32[8,128]{1,0:T(8,128)} %broadcast_in_dim.73.own_ref), custom_call_target="tpu_custom_call" | custom-call | tf_op jit(solution)/shard_map/sum_mesh/pallas_call | solution.py:220
  182.8 1.6 multiply_add_fusion.1
  184.9 1.6 slice_subtract_fusion
  (73 shorter events, 33.0 us)
Async XLA Ops:
  10.0 24.6 %all-to-all-start = ((bf16[16,160,128]{2,1,0:T(8,128)(2,1)}), bf16[16,160,128]{2,1,0:T(8,128)(2,1)S(1)}, u32[]{:S(2)}, u32[]{:S(2)}) async-start(bf16[16,160,128]{2,1,0:T(8,128)(2,1)} %pack.1), calls=%async_computation | async-start | bytes 1310720 | tf_op jit(solution)/shard_map/all_to_all | solution.py:301
  34.6 0.9 copy-start.4
  41.6 5.5 %collective-permute-start = (f32[32,544]{1,0:T(8,128)S(1)}, f32[32,544]{1,0:T(8,128)S(1)}, u32[]{:S(2)}, u32[]{:S(2)}) collective-permute-start(f32[32,544]{1,0:T(8,128)S(1)} %get-tuple-element.50), channel_id=1, source_target_pairs={{0,8},{8,16},{16,24},{1,9},{9,17},{17,25},{2,10},{10,18},{18,26},{... | collective-permute-start | bytes 208904 | tf_op jit(solution)/shard_map/ppermute | solution.py:264
  43.4 6.4 %collective-permute-start.1 = (f32[32,544]{1,0:T(8,128)S(1)}, f32[32,544]{1,0:T(8,128)S(1)}, u32[]{:S(2)}, u32[]{:S(2)}) collective-permute-start(f32[32,544]{1,0:T(8,128)S(1)} %get-tuple-element.51), channel_id=1, source_target_pairs={{8,0},{16,8},{24,16},{9,1},{17,9},{25,17},{10,2},{18,10},{26,18},{... | collective-permute-start | bytes 208904 | tf_op jit(solution)/shard_map/ppermute | solution.py:265
  51.0 9.8 %collective-permute-start.3 = (f32[136,128]{1,0:T(8,128)S(1)}, f32[136,128]{1,0:T(8,128)S(1)}, u32[]{:S(2)}, u32[]{:S(2)}) collective-permute-start(f32[136,128]{1,0:T(8,128)S(1)} %get-tuple-element.43), channel_id=1, source_target_pairs={{1,0},{2,1},{3,2},{4,3},{5,4},{6,5},{7,6},{9,8},{10,9},{11,10},{12... | collective-permute-start | bytes 208904 | tf_op jit(solution)/shard_map/ppermute | solution.py:261
  52.4 10.0 %collective-permute-start.2 = (f32[136,128]{1,0:T(8,128)S(1)}, f32[136,128]{1,0:T(8,128)S(1)}, u32[]{:S(2)}, u32[]{:S(2)}) collective-permute-start(f32[136,128]{1,0:T(8,128)S(1)} %get-tuple-element.42), channel_id=1, source_target_pairs={{0,1},{1,2},{2,3},{3,4},{4,5},{5,6},{6,7},{8,9},{9,10},{10,11},{11... | collective-permute-start | bytes 208904 | tf_op jit(solution)/shard_map/ppermute | solution.py:260
  71.6 10.4 %collective-permute-start.4 = (f32[32,544]{1,0:T(8,128)S(1)}, f32[32,544]{1,0:T(8,128)S(1)}, u32[]{:S(2)}, u32[]{:S(2)}) collective-permute-start(f32[32,544]{1,0:T(8,128)S(1)} %get-tuple-element.38), channel_id=1, source_target_pairs={{0,8},{8,16},{16,24},{1,9},{9,17},{17,25},{2,10},{10,18},{18,26},{... | collective-permute-start | bytes 208904 | tf_op jit(solution)/shard_map/ppermute | solution.py:264
  78.3 4.7 %collective-permute-start.5 = (f32[32,544]{1,0:T(8,128)S(1)}, f32[32,544]{1,0:T(8,128)S(1)}, u32[]{:S(2)}, u32[]{:S(2)}) collective-permute-start(f32[32,544]{1,0:T(8,128)S(1)} %get-tuple-element.39), channel_id=1, source_target_pairs={{8,0},{16,8},{24,16},{9,1},{17,9},{25,17},{10,2},{18,10},{26,18},{... | collective-permute-start | bytes 208904 | tf_op jit(solution)/shard_map/ppermute | solution.py:265
  84.2 14.1 %collective-permute-start.7 = (f32[136,128]{1,0:T(8,128)S(1)}, f32[136,128]{1,0:T(8,128)S(1)}, u32[]{:S(2)}, u32[]{:S(2)}) collective-permute-start(f32[136,128]{1,0:T(8,128)S(1)} %get-tuple-element.31), channel_id=1, source_target_pairs={{1,0},{2,1},{3,2},{4,3},{5,4},{6,5},{7,6},{9,8},{10,9},{11,10},{12... | collective-permute-start | bytes 208904 | tf_op jit(solution)/shard_map/ppermute | solution.py:261
  85.6 14.3 %collective-permute-start.6 = (f32[136,128]{1,0:T(8,128)S(1)}, f32[136,128]{1,0:T(8,128)S(1)}, u32[]{:S(2)}, u32[]{:S(2)}) collective-permute-start(f32[136,128]{1,0:T(8,128)S(1)} %get-tuple-element.30), channel_id=1, source_target_pairs={{0,1},{1,2},{2,3},{3,4},{4,5},{5,6},{6,7},{8,9},{9,10},{10,11},{11... | collective-permute-start | bytes 208904 | tf_op jit(solution)/shard_map/ppermute | solution.py:260
  100.6 1.1 copy-start
  138.2 7.4 %collective-permute-start.8 = (f32[32,544]{1,0:T(8,128)S(1)}, f32[32,544]{1,0:T(8,128)S(1)}, u32[]{:S(2)}, u32[]{:S(2)}) collective-permute-start(f32[32,544]{1,0:T(8,128)S(1)} %get-tuple-element.26), channel_id=1, source_target_pairs={{0,8},{8,16},{16,24},{1,9},{9,17},{17,25},{2,10},{10,18},{18,26},{... | collective-permute-start | bytes 208904 | tf_op jit(solution)/shard_map/ppermute | solution.py:264
  141.9 4.2 %collective-permute-start.9 = (f32[32,544]{1,0:T(8,128)S(1)}, f32[32,544]{1,0:T(8,128)S(1)}, u32[]{:S(2)}, u32[]{:S(2)}) collective-permute-start(f32[32,544]{1,0:T(8,128)S(1)} %get-tuple-element.27), channel_id=1, source_target_pairs={{8,0},{16,8},{24,16},{9,1},{17,9},{25,17},{10,2},{18,10},{26,18},{... | collective-permute-start | bytes 208904 | tf_op jit(solution)/shard_map/ppermute | solution.py:265
  147.3 12.3 %collective-permute-start.11 = (f32[136,128]{1,0:T(8,128)S(1)}, f32[136,128]{1,0:T(8,128)S(1)}, u32[]{:S(2)}, u32[]{:S(2)}) collective-permute-start(f32[136,128]{1,0:T(8,128)S(1)} %get-tuple-element.19), channel_id=1, source_target_pairs={{1,0},{2,1},{3,2},{4,3},{5,4},{6,5},{7,6},{9,8},{10,9},{11,10},{12... | collective-permute-start | bytes 208904 | tf_op jit(solution)/shard_map/ppermute | solution.py:261
  148.7 12.5 %collective-permute-start.10 = (f32[136,128]{1,0:T(8,128)S(1)}, f32[136,128]{1,0:T(8,128)S(1)}, u32[]{:S(2)}, u32[]{:S(2)}) collective-permute-start(f32[136,128]{1,0:T(8,128)S(1)} %get-tuple-element.18), channel_id=1, source_target_pairs={{0,1},{1,2},{2,3},{3,4},{4,5},{5,6},{6,7},{8,9},{9,10},{10,11},{11... | collective-permute-start | bytes 208904 | tf_op jit(solution)/shard_map/ppermute | solution.py:260
  161.9 1.1 copy-start.1
  182.8 1.6 copy-start.2
  182.8 2.1 %copy-start.3 = (f32[544,544]{1,0:T(8,128)S(1)}, f32[544,544]{1,0:T(8,128)}, u32[]{:S(2)}) copy-start(f32[544,544]{1,0:T(8,128)} %get-tuple-element.13) | copy-start | bytes 3551236
where the time goes:
time: 185 us; the launch traced here: 187 us
  starting transfers between devices  58.3 us (32%)
  Pallas kernels  51.9 us (28%)
  waiting for transfers between devices  25.8 us (14%)
  other arithmetic  23.3 us (13%)
  local copies, waits for them, and re-layouts  21.6 us (12%)
  between operations  5.61 us (3%)
    pallas_call x2, Pallas kernels, sum_over_mesh(): pl.pallas_call(functools.partial(sum_kernel, axes), out_shape=jax.ShapeDt...  31.3 us
    ppermute x3, starting transfers between devices, share_edges(): before = lax.ppermute(flat_strip(last), axis, up)  30.9 us
    all_to_all x1, waiting for transfers between devices, body(): lax.all_to_all(packed, 'tx', split_axis=0, concat_axis=0, tiled=True)  17.3 us
    pallas_call x2, Pallas kernels, body(): pl.pallas_call(functools.partial(normal_kernel, slot_count, per_row, bloc...  13.4 us
    ppermute x3, starting transfers between devices, share_edges(): before = lax.ppermute(last, axis, up)  12.3 us
    all_to_all x1, starting transfers between devices, body(): lax.all_to_all(packed, 'tx', split_axis=0, concat_axis=0, tiled=True)  7.31 us
    pallas_call x1, Pallas kernels, body(): pl.pallas_call(functools.partial(first_kernel, slot_count, per_row, block...  5.17 us
    slice x6, local copies, waits for them, and re-layouts, share_edges(): middle = lax.slice_in_dim(value, 2 * width, length - 2 * width, axis=dim)  5.16 us
  transfers between devices with their start and end apart: 13, of which 7 were waited for; matrix products, arithmetic and copies ran while one was open for 5% of the time, Pallas kernels for 0%

commit v1 on v0

v1 whole, which is shorter than its diff:
```python
import functools

import jax
import jax.numpy as jnp
from jax import lax
from jax.experimental import pallas as pl
from jax.experimental.pallas import tpu as pltpu
from jax.sharding import PartitionSpec as P

TILE = 512
SUB = 4
LANES = 128
GROUP = 32
MARGIN = 16
CAP = 2
EDGE = 2 * MARGIN
EXTENT = TILE + EDGE
PATCH = LANES + EDGE
ROWS = 144
PAD = 16
WIRE = jnp.bfloat16
SIDES = ((-1, 0), (1, 0), (0, -1), (0, 1), (-1, -1), (-1, 1), (1, -1), (1, 1))

damping = 0.05


def turn(value, shift):
    return pltpu.roll(value, shift % LANES, 1) if shift % LANES else value


def lanes_of(shape):
    return lax.broadcasted_iota(jnp.int32, shape, len(shape) - 1)


def pick_groups(parts):
    groups = lanes_of(parts[0].shape) >> 5
    value = parts[-1]
    for number in range(len(parts) - 2, -1, -1):
        value = jnp.where(groups == number, parts[number], value)
    return value


def make_taps(spread_ref, warp_ref, pad_ref, taps_ref, frame):
    pad_ref[frame] = jnp.zeros(pad_ref.shape[1:], jnp.float32)
    side = spread_ref.shape[1]
    pad_ref[frame, 8 : 8 + side, 0:side] = spread_ref[frame]
    shape = (GROUP, LANES)
    row_frac = jnp.full(shape, warp_ref[frame, 0], jnp.int32).astype(jnp.float32) / SUB
    col_frac = jnp.full(shape, warp_ref[frame, 1], jnp.int32).astype(jnp.float32) / SUB
    here = pad_ref[frame, 8 : 8 + GROUP]
    total = jnp.sum(jnp.sum(here, axis=0, keepdims=True), axis=1, keepdims=True)
    here = here / total
    above = pad_ref[frame, 7 : 7 + GROUP] / total
    here = (1.0 - col_frac) * here + col_frac * turn(here, 1)
    above = (1.0 - col_frac) * above + col_frac * turn(above, 1)
    pad_ref[frame, 8 : 8 + GROUP] = (1.0 - row_frac) * here + row_frac * above
    parts = []
    for part in range(4):
        near = pad_ref[frame, 8 + 8 * part : 12 + 8 * part]
        far = pad_ref[frame, 12 + 8 * part : 16 + 8 * part]
        parts.append(near + turn(far, 64))
    for part in range(4):
        pad_ref[frame, 8 + 4 * part : 12 + 4 * part] = parts[part]
    taps_ref[frame] = pad_ref[frame, 8:24].astype(jnp.bfloat16)


def toeplitz(rows):
    tiles = []
    for j in range(8):
        halves = []
        for half in range(2):
            row = rows[8 * half + j : 8 * half + j + 1]
            spread = jnp.broadcast_to(row, (GROUP, LANES))
            halves.append(pltpu.roll(spread, 0, 1, stride=1, stride_axis=0))
        tiles.append(jnp.concatenate(halves, axis=1))
    return jnp.concatenate(tiles, axis=0).astype(jnp.bfloat16)


def blur(shifted_ref, first, matrix, joined_ref):
    for g in range(4):
        near = shifted_ref[first + g, :ROWS]
        far = shifted_ref[first + g, PATCH - ROWS :]
        product = lax.dot_general(
            jnp.concatenate([near, far], axis=1),
            matrix,
            (((1,), (1,)), ((), ())),
            preferred_element_type=jnp.float32,
        )
        joined_ref[g] = product[: ROWS - 8, :LANES] + product[8:, LANES:]
    total = None
    for step in range(4):
        chosen = pick_groups([joined_ref[(j + step) % 4, j : j + LANES] for j in range(4)])
        chosen = turn(chosen, 32 * step)
        total = chosen if total is None else total + chosen
    return total


def hold_turns(image, turned_ref):
    for step in range(4):
        turned_ref[step, PAD : PAD + LANES] = turn(image, 32 * step)


def blur_back(turned_ref, matrix, behind_ref):
    low = lanes_of((PATCH, LANES)) < 64
    folded = []
    for h in range(4):
        rows = pick_groups(
            [turned_ref[(j - h) % 4, PAD - 8 - j : PAD - 8 - j + ROWS + 8] for j in range(4)]
        )
        stacked = jnp.concatenate(
            [rows[8:].astype(jnp.bfloat16), rows[:ROWS].astype(jnp.bfloat16)], axis=1
        )
        product = jnp.dot(stacked, matrix, preferred_element_type=jnp.float32)
        near, far = product[:, :LANES], product[:, LANES:]
        folded.append(jnp.concatenate([near[:16], near[16:] + far[: ROWS - 16], far[ROWS - 16 :]], axis=0))
    sums = []
    for number in range(2):
        one, two = folded[number], folded[number + 2]
        behind_ref[number, 8 : 8 + PATCH] = jnp.where(low, turn(one, 64), two)
        ahead = jnp.where(low, one, turn(two, 64))
        sums.append(ahead + behind_ref[number, 4 : 4 + PATCH])
    moved = turn(sums[1], 32)
    wrapped = lanes_of(moved.shape) < GROUP
    return sums[0] + jnp.where(wrapped, 0.0, moved), jnp.where(wrapped, moved, 0.0)


def assemble(running_ref, index_ref, per_row, field_ref):
    block = LANES

    def part(row, col, side, first, count):
        if 0 <= row < per_row and 0 <= col < per_row:
            return [running_ref[index_ref[row * per_row + col], side, first : first + count]]
        return []

    for row in range(per_row + 1):
        for col in range(per_row + 1):
            both = part(row - 1, col, 0, block, EDGE) + part(row - 1, col - 1, 1, block, EDGE)
            rest = part(row, col, 0, 0, EDGE) + part(row, col - 1, 1, 0, EDGE)
            field_ref[col, row * block : row * block + EDGE] = sum((both + rest)[1:], (both + rest)[0])
            if row < per_row:
                count = block - EDGE
                body = part(row, col, 0, EDGE, count) + part(row, col - 1, 1, EDGE, count)
                field_ref[col, row * block + EDGE : (row + 1) * block] = sum(body[1:], body[0])


def flat_strip(strip_ref, tile):
    height = EXTENT // 4
    parts = [turn(strip_ref[tile, k * height : (k + 1) * height], 32 * k) for k in range(4)]
    return pick_groups(parts).astype(WIRE)


def add_flat(field_ref, tile, flat):
    height = EXTENT // 4
    wrapped = lanes_of((height, LANES)) < GROUP
    flat = flat.astype(jnp.float32)
    for k in range(4):
        rows = slice(k * height, (k + 1) * height)
        field_ref[tile, rows] += jnp.where(wrapped, turn(flat, -32 * k), 0.0)


def shift_field(field_ref, shifted_ref, per_row, sums_ref, row):
    chunk = 16

    tall = PATCH // chunk

    @pl.loop(0, per_row * tall)
    def _(step):
        number = step // tall * (LANES // chunk) + lax.rem(step, tall)
        start = pl.multiple_of(number * chunk, chunk)
        local = pl.multiple_of(lax.rem(step, tall) * chunk, chunk)
        cell = step // tall * per_row
        lanes = lanes_of((chunk, LANES))
        low, middle = lanes < 64, (lanes >= 32) & (lanes < 96)
        now = [field_ref[col, pl.ds(start, chunk)] for col in range(per_row + 1)]
        later = [field_ref[col, pl.ds(start + 4, chunk)] for col in range(per_row + 1)]
        by96 = [turn(jnp.where(middle, a, b), 96) for a, b in zip(now, later)]
        by32 = [turn(jnp.where(middle, b, a), 32) for a, b in zip(now, later)]
        for col in range(per_row):
            a, b = now[col], later[col]
            by64 = turn(jnp.where(low, b, a), 64)
            parts = [
                jnp.where(low, a, by64),
                jnp.where(low, by96[col], by32[col]),
                jnp.where(low, by64, b),
                pick_groups([by32[col], by32[col + 1], by96[col], by96[col + 1]]),
            ]
            for g in range(4):
                shifted_ref[4 * (cell + col) + g, pl.ds(local, chunk)] = parts[g].astype(jnp.bfloat16)
        squares = None
        for col in range(per_row + 1):
            value = now[col]
            if col == 0:
                value = jnp.where(lanes < MARGIN, 0.0, value)
            if col == per_row:
                value = jnp.where(lanes < MARGIN, value, 0.0)
            squares = value * value if squares is None else squares + value * value
        once = (lax.rem(step, tall) < LANES // chunk) | (cell == per_row * (per_row - 1))
        inside = once & (number >= MARGIN // chunk) & (number < EXTENT // chunk - MARGIN // chunk)
        sums_ref[row] += jnp.where(inside, squares[:8] + squares[8:], 0.0)


def whole_kernel(
    sizes,
    exposures_ref,
    spread_ref,
    warp_ref,
    column_ref,
    cell_ref,
    solution_ref,
    residual_ref,
    pad_ref,
    taps_ref,
    send_ref,
    frames_ref,
    tag_send_ref,
    tags_ref,
    tag_smem,
    key_smem,
    order_smem,
    index_smem,
    matrix_ref,
    patch_ref,
    running_ref,
    turned_ref,
    behind_ref,
    joined_ref,
    shifted_ref,
    field_ref,
    row_send_ref,
    col_send_ref,
    row_land_ref,
    col_land_ref,
    corner_land_ref,
    sums_ref,
    total_ref,
    ty_land_ref,
    tx_land_ref,
    tag_sems,
    frame_sems,
    local_sem,
    halo_sems,
    ty_sems,
    tx_sems,
):
    ty_size, tx_size = sizes
    frame_count, block = exposures_ref.shape[:2]
    per_row = TILE // block
    cells = per_row * per_row
    slots = CAP * tx_size
    ty, tx = lax.axis_index("ty"), lax.axis_index("tx")

    def has(side):
        row, col = side
        ok = None
        for step, place, size in ((row, ty, ty_size), (col, tx, tx_size)):
            test = (place > 0) if step < 0 else (place < size - 1) if step > 0 else None
            if test is not None:
                ok = test if ok is None else ok & test
        return ok

    def at(side):
        return {"ty": ty + side[0], "tx": tx + side[1]}

    barrier = pltpu.get_barrier_semaphore()

    def greet(device):
        pl.semaphore_signal(barrier, inc=1, device_id=device, device_id_type=pl.DeviceIdType.MESH)

    for step in range(1, tx_size):
        greet({"tx": lax.rem(tx + step, tx_size)})
    for step in range(1, ty_size):
        greet({"ty": lax.rem(ty + step, ty_size)})
    for side in SIDES[4:]:
        pl.when(has(side))(functools.partial(greet, at(side)))

    for frame in range(frame_count):
        make_taps(spread_ref, warp_ref, pad_ref, taps_ref, frame)

    running_ref[0] = jnp.zeros(running_ref.shape[1:], jnp.float32)
    turned_ref[...] = jnp.zeros_like(turned_ref)
    behind_ref[...] = jnp.zeros_like(behind_ref)
    sums_ref[...] = jnp.zeros_like(sums_ref)
    for number in range(3):
        field_ref[number, :, EXTENT:] = jnp.zeros((per_row + 1, 8, LANES), jnp.float32)

    peers = tx_size - 1 + ty_size - 1
    for side in SIDES[4:]:
        peers = peers + jnp.where(has(side), 1, 0)
    pl.semaphore_wait(barrier, peers)

    def sources(target):
        first, second, count = jnp.int32(0), jnp.int32(0), jnp.int32(0)
        for frame in range(frame_count):
            match = column_ref[frame_count - 1 - frame] == target
            first = jnp.where(match, frame_count - 1 - frame, first)
            second = jnp.where(column_ref[frame] == target, frame, second)
            count = count + jnp.where(match, 1, 0)
        return first, second, count

    def tag_copy(step):
        return pltpu.make_async_remote_copy(
            src_ref=tag_send_ref.at[step],
            dst_ref=tags_ref.at[step],
            send_sem=tag_sems.at[0, step],
            recv_sem=tag_sems.at[1, step],
            device_id={"tx": lax.rem(tx + step, tx_size)},
            device_id_type=pl.DeviceIdType.MESH,
        )

    def frame_copy(step):
        return pltpu.make_async_remote_copy(
            src_ref=send_ref.at[step],
            dst_ref=frames_ref.at[step],
            send_sem=frame_sems.at[0, step],
            recv_sem=frame_sems.at[1, step],
            device_id={"tx": lax.rem(tx + step, tx_size)},
            device_id_type=pl.DeviceIdType.MESH,
        )

    def tags_for(step):
        first, second, count = sources(lax.rem(tx + step, tx_size))
        one = jnp.where(count >= 1, cell_ref[first], -1)
        two = jnp.where(count >= 2, cell_ref[second], -1)
        shape = tags_ref.shape[1:]
        rows = lax.broadcasted_iota(jnp.int32, shape, 0)
        return jnp.where(rows == 0, jnp.full(shape, one, jnp.int32), jnp.full(shape, two, jnp.int32))

    def fill(ref, step):
        first, second, _ = sources(lax.rem(tx + step, tx_size))
        for number, origin in enumerate((first, second)):
            ref[step, number, :block] = exposures_ref[origin].astype(jnp.bfloat16)
            ref[step, number, block:] = taps_ref[origin]

    tags_ref[0] = tags_for(0)

    @pl.loop(1, tx_size)
    def _(step):
        tag_send_ref[step] = tags_for(step)
        tag_copy(step).start()

    @pl.loop(1, tx_size)
    def _(step):
        fill(send_ref, step)
        frame_copy(step).start()

    fill(frames_ref, 0)

    def first_pass(step):
        for number in range(CAP):
            slot = CAP * step + number
            matrix = toeplitz(frames_ref[step, number, block:].astype(jnp.float32))
            matrix_ref[slot] = matrix
            hold_turns(frames_ref[step, number, :block].astype(jnp.float32), turned_ref)
            left, right = blur_back(turned_ref, matrix, behind_ref)
            patch_ref[slot, 0] = left
            patch_ref[slot, 1] = right

    first_pass(0)

    @pl.loop(1, tx_size)
    def _(step):
        tag_copy(step).wait()

    local = pltpu.make_async_copy(tags_ref, tag_smem, local_sem)
    local.start()
    local.wait()

    @pl.loop(0, slots)
    def _(slot):
        key_smem[slot] = tag_smem[slot // CAP, lax.rem(slot, CAP), 0] * slots + slot

    @pl.loop(0, slots)
    def _(slot):
        key = key_smem[slot]
        rank = jnp.int32(0)
        for other in range(slots):
            rank = rank + jnp.where(key_smem[other] < key, 1, 0)
        order_smem[0, slot] = rank

    @pl.loop(0, slots)
    def _(place):
        slot = jnp.int32(0)
        for other in range(slots):
            slot = jnp.where(order_smem[0, other] == place, other, slot)
        order_smem[1, place] = slot
        cell = tag_smem[slot // CAP, lax.rem(slot, CAP), 0]
        order_smem[2, place] = cell

    @pl.loop(0, cells)
    def _(cell):
        upto, equal = jnp.int32(0), jnp.int32(0)
        for place in range(slots):
            value = order_smem[2, place]
            upto = upto + jnp.where(value <= cell, 1, 0)
            equal = equal + jnp.where(value == cell, 1, 0)
        index_smem[cell] = jnp.where(equal > 0, upto, 0)

    @pl.loop(1, tx_size)
    def _(step):
        frame_copy(step).wait()
        first_pass(step)

    def same(place):
        before = order_smem[2, jnp.maximum(place - 1, 0)]
        return (place > 0) & (before == order_smem[2, place])

    @pl.loop(0, slots)
    def _(place):
        kept = same(place)
        slot = order_smem[1, place]
        for side in range(2):
            running_ref[place + 1, side] = patch_ref[slot, side] + jnp.where(
                kept, running_ref[place, side], 0.0
            )

    def halo_copy(turn_number, which):
        row, col = SIDES[which]
        if col == 0:
            source = row_send_ref.at[turn_number, (row + 1) // 2]
            target = row_land_ref.at[turn_number, (1 - row) // 2]
        elif row == 0:
            source = col_send_ref.at[turn_number, (col + 1) // 2]
            target = col_land_ref.at[turn_number, (1 - col) // 2]
        else:
            source = row_send_ref.at[turn_number, (row + 1) // 2, per_row * ((col + 1) // 2)]
            target = corner_land_ref.at[turn_number, (1 - row) // 2, (1 - col) // 2]
        return pltpu.make_async_remote_copy(
            src_ref=source,
            dst_ref=target,
            send_sem=halo_sems.at[0, turn_number, which],
            recv_sem=halo_sems.at[1, turn_number, SIDES.index((-row, -col))],
            device_id=at(SIDES[which]),
            device_id_type=pl.DeviceIdType.MESH,
        )

    def share_edges(number):
        own = field_ref.at[number]
        for end in range(2):
            col_send_ref[number, end] = flat_strip(own, per_row * end)
        for which in (2, 3):
            pl.when(has(SIDES[which]))(lambda which=which: halo_copy(number, which).start())
        for end in range(2):
            for col in range(per_row + 1):
                row_send_ref[number, end, col] = own[col, TILE * end : TILE * end + EDGE].astype(WIRE)
        for which in (4, 5, 6, 7, 0, 1):
            pl.when(has(SIDES[which]))(lambda which=which: halo_copy(number, which).start())

    def take_edges(number):
        own = field_ref.at[number]

        def land(which):
            row, col = SIDES[which]
            halo_copy(number, which).wait_send()
            back = SIDES.index((row, col))
            pltpu.make_async_remote_copy(
                src_ref=halo_source(which),
                dst_ref=halo_target(which),
                send_sem=halo_sems.at[0, number, which],
                recv_sem=halo_sems.at[1, number, back],
                device_id=at(SIDES[which]),
                device_id_type=pl.DeviceIdType.MESH,
            ).wait_recv()
            if col == 0:
                end = (row + 1) // 2
                for tile in range(per_row + 1):
                    own[tile, TILE * end : TILE * end + EDGE] += row_land_ref[number, end, tile].astype(
                        jnp.float32
                    )
            elif row == 0:
                end = (col + 1) // 2
                add_flat(own, per_row * end, col_land_ref[number, end])
            else:
                end, tile = (row + 1) // 2, per_row * ((col + 1) // 2)
                value = corner_land_ref[number, end, (col + 1) // 2].astype(jnp.float32)
                inside = lanes_of(value.shape) < EDGE
                own[tile, TILE * end : TILE * end + EDGE] += jnp.where(inside, value, 0.0)

        def halo_source(which):
            row, col = SIDES[which]
            if col == 0:
                return row_send_ref.at[number, (row + 1) // 2]
            if row == 0:
                return col_send_ref.at[number, (col + 1) // 2]
            return row_send_ref.at[number, (row + 1) // 2, per_row * ((col + 1) // 2)]

        def halo_target(which):
            row, col = SIDES[which]
            if col == 0:
                return row_land_ref.at[number, (row + 1) // 2]
            if row == 0:
                return col_land_ref.at[number, (col + 1) // 2]
            return corner_land_ref.at[number, (row + 1) // 2, (col + 1) // 2]

        for which in range(len(SIDES)):
            pl.when(has(SIDES[which]))(functools.partial(land, which))

    def clear_outside(number):
        own = field_ref.at[number]

        @pl.when(ty == 0)
        def _():
            for tile in range(per_row + 1):
                own[tile, :MARGIN] = jnp.zeros((MARGIN, LANES), jnp.float32)

        @pl.when(ty == ty_size - 1)
        def _():
            for tile in range(per_row + 1):
                own[tile, TILE + MARGIN : EXTENT] = jnp.zeros((MARGIN, LANES), jnp.float32)

        @pl.when(tx == 0)
        def _():
            value = own[0, :EXTENT]
            own[0, :EXTENT] = jnp.where(lanes_of(value.shape) < MARGIN, 0.0, value)

        @pl.when(tx == tx_size - 1)
        def _():
            value = own[per_row, :EXTENT]
            own[per_row, :EXTENT] = jnp.where(lanes_of(value.shape) < MARGIN, value, 0.0)

    def gather_field(number):
        assemble(running_ref, index_smem, per_row, field_ref.at[number])
        share_edges(number)

    def damp(number):
        for tile in range(per_row + 1):
            field_ref[number, tile, :EXTENT] += damping * field_ref[number - 1, tile, :EXTENT]

    def normal_pass(row):
        @pl.loop(0, slots)
        def _(place):
            slot = order_smem[1, place]
            cell = order_smem[2, place]
            valid = cell >= 0
            cell = jnp.maximum(cell, 0)
            kept = same(place)
            matrix = matrix_ref[slot]
            modelled = blur(shifted_ref, cell * 4, matrix, joined_ref)
            squares = modelled * modelled
            squares = squares.reshape(block // 8, 8, LANES).sum(axis=0)
            sums_ref[row] += jnp.where(valid, squares, 0.0)
            hold_turns(modelled.astype(jnp.bfloat16).astype(jnp.float32), turned_ref)
            left, right = blur_back(turned_ref, matrix, behind_ref)
            running_ref[place + 1, 0] = left + jnp.where(kept, running_ref[place, 0], 0.0)
            running_ref[place + 1, 1] = right + jnp.where(kept, running_ref[place, 1], 0.0)

    gather_field(0)
    take_edges(0)
    clear_outside(0)
    shift_field(field_ref.at[0], shifted_ref, per_row, sums_ref, 0)
    normal_pass(1)
    gather_field(1)
    take_edges(1)
    clear_outside(1)
    damp(1)
    shift_field(field_ref.at[1], shifted_ref, per_row, sums_ref, 2)
    normal_pass(3)

    def sum_copies(axis, place, size, source, landed, sems):
        return [
            pltpu.make_async_remote_copy(
                src_ref=source,
                dst_ref=landed.at[step - 1],
                send_sem=sems.at[0, step - 1],
                recv_sem=sems.at[1, step - 1],
                device_id={axis: lax.rem(place + step, size)},
                device_id_type=pl.DeviceIdType.MESH,
            )
            for step in range(1, size)
        ]

    rows = lax.broadcasted_iota(jnp.int32, (8, LANES), 0)
    packed = jnp.zeros((8, LANES), jnp.float32)
    for number in range(4):
        packed = jnp.where(rows == number, jnp.sum(sums_ref[number], axis=0, keepdims=True), packed)
    total_ref[0] = packed
    ty_copies = sum_copies("ty", ty, ty_size, total_ref.at[0], ty_land_ref, ty_sems)
    for copy in ty_copies:
        copy.start()
    assemble(running_ref, index_smem, per_row, field_ref.at[2])
    share_edges(2)
    for copy in ty_copies:
        copy.wait()
    partial = total_ref[0]
    for step in range(ty_size - 1):
        partial = partial + ty_land_ref[step]
    total_ref[1] = partial
    tx_copies = sum_copies("tx", tx, tx_size, total_ref.at[1], tx_land_ref, tx_sems)
    for copy in tx_copies:
        copy.start()
    take_edges(2)
    damp(2)
    for copy in tx_copies:
        copy.wait()
    partial = total_ref[1]
    for step in range(tx_size - 1):
        partial = partial + tx_land_ref[step]
    sums = jnp.broadcast_to(jnp.sum(partial, axis=1, keepdims=True), (8, LANES))
    r00 = sums[0:1]
    r01 = sums[1:2] + damping * r00
    r11 = sums[2:3]
    r12 = sums[3:4] + damping * r11
    step0 = r00 / r01
    norm_next = r00 - 2.0 * step0 * r01 + step0 * step0 * r11
    grown = 1.0 + norm_next / r00
    curvature = grown * grown * r01 - 2.0 * grown * step0 * r11 + step0 * step0 * r12
    step1 = norm_next / curvature
    x0 = step0 + step1 * grown
    x1 = -step1 * step0
    y1 = -step0 - step1 * grown
    y2 = step1 * step0

    chunk = 32

    @pl.loop(0, TILE // chunk)
    def _(number):
        start = pl.multiple_of(number * chunk, chunk)
        source = pl.ds(pl.multiple_of(start + MARGIN, 8), chunk)
        inside = lanes_of((chunk, LANES)) < LANES - MARGIN
        solved, left = [], []
        for tile in range(per_row + 1):
            q0, q1, q2 = (field_ref[k, tile, source] for k in range(3))
            solved.append(turn(x0 * q0 + x1 * q1, -MARGIN))
            left.append(turn(q0 + y1 * q1 + y2 * q2, -MARGIN))
        for tile in range(per_row):
            lanes = slice(tile * LANES, (tile + 1) * LANES)
            solution_ref[pl.ds(start, chunk), lanes] = jnp.where(inside, solved[tile], solved[tile + 1])
            residual_ref[pl.ds(start, chunk), lanes] = jnp.where(inside, left[tile], left[tile + 1])


def body(exposures, point_spread, warp_steps, column, block_cell):
    ty_size, tx_size = lax.axis_size("ty"), lax.axis_size("tx")
    frame_count, block = exposures.shape[:2]
    per_row = TILE // block
    slots = CAP * tx_size
    tall = EXTENT + 8
    f32, bf16 = jnp.float32, jnp.bfloat16
    vmem = pl.BlockSpec(memory_space=pltpu.VMEM)
    smem = pl.BlockSpec(memory_space=pltpu.SMEM)
    dma = pltpu.SemaphoreType.DMA
    scratch = [
        pltpu.VMEM((frame_count, 48, LANES), f32),
        pltpu.VMEM((frame_count, 16, LANES), bf16),
        pltpu.VMEM((tx_size, CAP, ROWS, LANES), bf16),
        pltpu.VMEM((tx_size, CAP, ROWS, LANES), bf16),
        pltpu.VMEM((tx_size, 8, LANES), jnp.int32),
        pltpu.VMEM((tx_size, 8, LANES), jnp.int32),
        pltpu.SMEM((tx_size, 8, LANES), jnp.int32),
        pltpu.SMEM((slots,), jnp.int32),
        pltpu.SMEM((3, slots), jnp.int32),
        pltpu.SMEM((per_row * per_row,), jnp.int32),
        pltpu.VMEM((slots, 256, 256), bf16),
        pltpu.VMEM((slots, 2, PATCH, LANES), f32),
        pltpu.VMEM((slots + 1, 2, PATCH, LANES), f32),
        pltpu.VMEM((4, PAD + ROWS, LANES), f32),
        pltpu.VMEM((2, 8 + PATCH, LANES), f32),
        pltpu.VMEM((4, ROWS - 8, LANES), f32),
        pltpu.VMEM((4 * per_row * per_row, PATCH, LANES), bf16),
        pltpu.VMEM((3, per_row + 1, tall, LANES), f32),
        pltpu.VMEM((3, 2, per_row + 1, EDGE, LANES), WIRE),
        pltpu.VMEM((3, 2, EXTENT // 4, LANES), WIRE),
        pltpu.VMEM((3, 2, per_row + 1, EDGE, LANES), WIRE),
        pltpu.VMEM((3, 2, EXTENT // 4, LANES), WIRE),
        pltpu.VMEM((3, 2, 2, EDGE, LANES), WIRE),
        pltpu.VMEM((4, 8, LANES), f32),
        pltpu.VMEM((2, 8, LANES), f32),
        pltpu.VMEM((ty_size - 1, 8, LANES), f32),
        pltpu.VMEM((tx_size - 1, 8, LANES), f32),
        dma((2, tx_size)),
        dma((2, tx_size)),
        dma,
        dma((2, 3, len(SIDES))),
        dma((2, ty_size - 1)),
        dma((2, tx_size - 1)),
    ]
    return pl.pallas_call(
        functools.partial(whole_kernel, (ty_size, tx_size)),
        out_shape=(jax.ShapeDtypeStruct((TILE, TILE), f32), jax.ShapeDtypeStruct((TILE, TILE), f32)),
        in_specs=[vmem, vmem, smem, smem, smem],
        out_specs=(vmem, vmem),
        scratch_shapes=scratch,
        compiler_params=pltpu.CompilerParams(collective_id=0, has_side_effects=True),
        name="whole",
    )(exposures, point_spread, warp_steps, column[:, 0], block_cell)


def solution(mesh):
    placed = (
        P(("ty", "tx"), None, None),
        P(("ty", "tx"), None, None),
        P(("ty", "tx"), None),
        P(("ty", "tx"), None),
        P(("ty", "tx")),
    )
    return jax.shard_map(
        body, mesh=mesh, in_specs=placed, out_specs=(P("ty", "tx"), P("ty", "tx")), check_vma=False
    )
```

time: 185 us -> 84.2 us (0.46)
  starting transfers between devices: 58.3 us -> 0 us
  waiting for transfers between devices: 25.8 us -> 0 us
  Pallas kernels: 51.9 us -> 77.1 us
  other arithmetic: 23.3 us -> 0 us
  local copies, waits for them, and re-layouts: 21.6 us -> 6.25 us
  between operations: 5.61 us -> 0.66 us
    ppermute x12 -> x0, starting transfers between devices: 51 us -> none  [the longest x3 30.9 us: share_edges(): before = lax.ppermute(flat_strip(last), axis, up)]
    pallas_call x6 -> x1, Pallas kernels: 51.9 us -> 77.1 us  [body(): pl.pallas_call(functools.partial(whole_kernel, (ty_size, tx_size)), out_s...]
    all_to_all x1 -> x0, waiting for transfers between devices: 17.3 us -> none  [body(): lax.all_to_all(packed, 'tx', split_axis=0, concat_axis=0, tiled=True)]
    slice x20 -> x0, local copies, waits for them, and re-layouts: 14.3 us -> none  [the longest x6 5.16 us: share_edges(): middle = lax.slice_in_dim(value, 2 * width, length - 2 * width, axis=dim)]
    ppermute x12 -> x0, waiting for transfers between devices: 8.53 us -> none  [the longest x3 4.32 us: share_edges(): before = lax.ppermute(flat_strip(last), axis, up)]
    all_to_all x1 -> x0, starting transfers between devices: 7.31 us -> none  [body(): lax.all_to_all(packed, 'tx', split_axis=0, concat_axis=0, tiled=True)]
    reduce_sum x5 -> x0, other arithmetic: 5.1 us -> none  [the longest x2 2.53 us: products(): return tuple((jnp.sum(inner(left * right)) for left, right in pairs))]
    convert_element_type x4 -> x0, other arithmetic: 3.82 us -> none  [the longest x2 3.13 us: body(): direction.astype(jnp.bfloat16)]
  transfers between devices with their start and end apart: 13 -> 0, of which waited for: 7 -> 0; matrix products, arithmetic and copies ran while one was open for 5% -> 0% of each run, Pallas kernels for 0% -> 0%
where the time goes in v1:
time: 84.2 us; the launch traced here: 84 us
  Pallas kernels  77.1 us (92%)
  local copies, waits for them, and re-layouts  6.25 us (7%)
    pallas_call x1, Pallas kernels, body(): pl.pallas_call(functools.partial(whole_kernel, (ty_size, tx_size)), out_s...  77.1 us
    unnamed x8, local copies, waits for them, and re-layouts  6.25 us

profile of v1, /device:TPU:0, one launch (start us, length us, event | category | flops | bytes accessed | tf_op | source)
XLA Modules:
  0.0 84.0 jit_solution(6787242220293714790)
XLA Ops:
  0.6 0.0 copy-start.1
  0.6 0.7 copy-done.1
  1.3 0.7 copy.8.warp_ref
  2.0 1.6 %copy.7.spread_ref = f32[8,31,31]{2,1,0:T(8,128)} copy(f32[8,31,31]{2,0,1:T(8,128)} %param.6) | data formatting | bytes 61504 | tf_op args[1]
  3.6 77.1 %whole.1 = (f32[512,512]{1,0:T(8,128)}, f32[512,512]{1,0:T(8,128)}) custom-call(f32[8,128,128]{2,1,0:T(8,128)} %exposures_ref.1, f32[8,31,31]{2,1,0:T(8,128)} %copy.7.spread_ref, s32[8,2]{1,0:T(8,128)} %copy.8.warp_ref, s32[8]{0:T(128)} %bitcast.1, s32[8]{0:T(128)} %cell_ref.1), custom_call_target="tpu_custom_call" | custom-call | tf_op jit(solution)/shard_map/whole/pallas_call | solution.py:675
  80.6 0.0 copy-start
  80.6 2.4 %copy.11 = f32[512,512]{1,0:T(8,128)} copy(f32[512,512]{1,0:T(8,128)} %get-tuple-element.4) | data formatting | bytes 2097152
  83.0 0.0 copy-done
  83.0 1.0 %copy.12 = f32[512,512]{1,0:T(8,128)} copy(f32[512,512]{1,0:T(8,128)S(1)} %copy-done) | data formatting | bytes 2097152
Async XLA Ops:
  0.6 0.7 copy-start.1
  80.6 2.4 %copy-start = (f32[512,512]{1,0:T(8,128)S(1)}, f32[512,512]{1,0:T(8,128)}, u32[]{:S(2)}) copy-start(f32[512,512]{1,0:T(8,128)} %get-tuple-element.5) | copy-start | bytes 3145732

commit v2 on v1

--- a/solution.py
+++ b/solution.py
@@ -40,28 +40,33 @@
     return value
 
 
-def make_taps(spread_ref, warp_ref, pad_ref, taps_ref, frame):
-    pad_ref[frame] = jnp.zeros(pad_ref.shape[1:], jnp.float32)
-    side = spread_ref.shape[1]
-    pad_ref[frame, 8 : 8 + side, 0:side] = spread_ref[frame]
-    shape = (GROUP, LANES)
-    row_frac = jnp.full(shape, warp_ref[frame, 0], jnp.int32).astype(jnp.float32) / SUB
-    col_frac = jnp.full(shape, warp_ref[frame, 1], jnp.int32).astype(jnp.float32) / SUB
-    here = pad_ref[frame, 8 : 8 + GROUP]
-    total = jnp.sum(jnp.sum(here, axis=0, keepdims=True), axis=1, keepdims=True)
-    here = here / total
-    above = pad_ref[frame, 7 : 7 + GROUP] / total
-    here = (1.0 - col_frac) * here + col_frac * turn(here, 1)
-    above = (1.0 - col_frac) * above + col_frac * turn(above, 1)
-    pad_ref[frame, 8 : 8 + GROUP] = (1.0 - row_frac) * here + row_frac * above
-    parts = []
-    for part in range(4):
-        near = pad_ref[frame, 8 + 8 * part : 12 + 8 * part]
-        far = pad_ref[frame, 12 + 8 * part : 16 + 8 * part]
-        parts.append(near + turn(far, 64))
-    for part in range(4):
-        pad_ref[frame, 8 + 4 * part : 12 + 4 * part] = parts[part]
-    taps_ref[frame] = pad_ref[frame, 8:24].astype(jnp.bfloat16)
+def make_taps(spread_ref, warp_ref, held_ref, taps_ref):
+    side, frames = spread_ref.shape[:2]
+    shape = (frames, LANES)
+    index = lax.broadcasted_iota(jnp.int32, shape, 0)
+    steps = [jnp.zeros(shape, jnp.int32), jnp.zeros(shape, jnp.int32)]
+    for which in range(2):
+        for frame in range(frames):
+            steps[which] = jnp.where(index == frame, warp_ref[which, frame], steps[which])
+    row_frac, col_frac = (step.astype(jnp.float32) / SUB for step in steps)
+    held_ref[...] = jnp.zeros_like(held_ref)
+    held_ref[:side, :frames, :side] = spread_ref[...]
+    points = [held_ref[a, :frames] for a in range(side)]
+    total = points[0]
+    for point in points[1:]:
+        total = total + point
+    total = jnp.sum(total, axis=1, keepdims=True)
+    points = [point / total for point in points] + [jnp.zeros(shape, jnp.float32)]
+    points = [(1.0 - col_frac) * point + col_frac * turn(point, 1) for point in points]
+    kernel = [(1.0 - row_frac) * points[0]]
+    for a in range(1, side + 1):
+        kernel.append((1.0 - row_frac) * points[a] + row_frac * points[a - 1])
+    for row in range(16):
+        a = row // 4 * 8 + row % 4
+        held_ref[row, :frames] = kernel[a] + turn(kernel[a + 4], 64)
+    for frame in range(frames):
+        rows = [held_ref[row, frame : frame + 1] for row in range(16)]
+        taps_ref[frame] = jnp.concatenate(rows, axis=0).astype(jnp.bfloat16)
 
 
 def toeplitz(rows):
@@ -195,8 +200,10 @@
                 value = jnp.where(lanes < MARGIN, value, 0.0)
             squares = value * value if squares is None else squares + value * value
         once = (lax.rem(step, tall) < LANES // chunk) | (cell == per_row * (per_row - 1))
-        inside = once & (number >= MARGIN // chunk) & (number < EXTENT // chunk - MARGIN // chunk)
-        sums_ref[row] += jnp.where(inside, squares[:8] + squares[8:], 0.0)
+        place = start + lax.broadcasted_iota(jnp.int32, squares.shape, 0)
+        squares = jnp.where((place >= MARGIN) & (place < EXTENT - MARGIN), squares, 0.0)
+        squares = squares.reshape(chunk // 8, 8, LANES).sum(axis=0)
+        sums_ref[row] += jnp.where(once, squares, 0.0)
 
 
 def whole_kernel(
@@ -233,14 +240,12 @@
     corner_land_ref,
     sums_ref,
     total_ref,
-    ty_land_ref,
-    tx_land_ref,
+    total_land_ref,
     tag_sems,
     frame_sems,
     local_sem,
     halo_sems,
-    ty_sems,
-    tx_sems,
+    sum_sems,
 ):
     ty_size, tx_size = sizes
     frame_count, block = exposures_ref.shape[:2]
@@ -266,15 +271,12 @@
     def greet(device):
         pl.semaphore_signal(barrier, inc=1, device_id=device, device_id_type=pl.DeviceIdType.MESH)
 
-    for step in range(1, tx_size):
-        greet({"tx": lax.rem(tx + step, tx_size)})
-    for step in range(1, ty_size):
-        greet({"ty": lax.rem(ty + step, ty_size)})
-    for side in SIDES[4:]:
-        pl.when(has(side))(functools.partial(greet, at(side)))
-
-    for frame in range(frame_count):
-        make_taps(spread_ref, warp_ref, pad_ref, taps_ref, frame)
+    @pl.loop(1, ty_size * tx_size)
+    def _(step):
+        peer = lax.rem(ty * tx_size + tx + step, ty_size * tx_size)
+        greet({"ty": peer // tx_size, "tx": lax.rem(peer, tx_size)})
+
+    make_taps(spread_ref, warp_ref, pad_ref, taps_ref)
 
     running_ref[0] = jnp.zeros(running_ref.shape[1:], jnp.float32)
     turned_ref[...] = jnp.zeros_like(turned_ref)
@@ -283,10 +285,7 @@
     for number in range(3):
         field_ref[number, :, EXTENT:] = jnp.zeros((per_row + 1, 8, LANES), jnp.float32)
 
-    peers = tx_size - 1 + ty_size - 1
-    for side in SIDES[4:]:
-        peers = peers + jnp.where(has(side), 1, 0)
-    pl.semaphore_wait(barrier, peers)
+    pl.semaphore_wait(barrier, ty_size * tx_size - 1)
 
     def sources(target):
         first, second, count = jnp.int32(0), jnp.int32(0), jnp.int32(0)
@@ -350,8 +349,8 @@
             slot = CAP * step + number
             matrix = toeplitz(frames_ref[step, number, block:].astype(jnp.float32))
             matrix_ref[slot] = matrix
-            hold_turns(frames_ref[step, number, :block].astype(jnp.float32), turned_ref)
-            left, right = blur_back(turned_ref, matrix, behind_ref)
+            hold_turns(frames_ref[step, number, :block].astype(jnp.float32), turned_ref.at[number])
+            left, right = blur_back(turned_ref.at[number], matrix, behind_ref.at[number])
             patch_ref[slot, 0] = left
             patch_ref[slot, 1] = right
 
@@ -525,80 +524,92 @@
         for tile in range(per_row + 1):
             field_ref[number, tile, :EXTENT] += damping * field_ref[number - 1, tile, :EXTENT]
 
-    def normal_pass(row):
-        @pl.loop(0, slots)
-        def _(place):
-            slot = order_smem[1, place]
-            cell = order_smem[2, place]
-            valid = cell >= 0
-            cell = jnp.maximum(cell, 0)
-            kept = same(place)
-            matrix = matrix_ref[slot]
-            modelled = blur(shifted_ref, cell * 4, matrix, joined_ref)
-            squares = modelled * modelled
-            squares = squares.reshape(block // 8, 8, LANES).sum(axis=0)
-            sums_ref[row] += jnp.where(valid, squares, 0.0)
-            hold_turns(modelled.astype(jnp.bfloat16).astype(jnp.float32), turned_ref)
-            left, right = blur_back(turned_ref, matrix, behind_ref)
-            running_ref[place + 1, 0] = left + jnp.where(kept, running_ref[place, 0], 0.0)
-            running_ref[place + 1, 1] = right + jnp.where(kept, running_ref[place, 1], 0.0)
+    def forward(row, place, lane):
+        cell = order_smem[2, place]
+        matrix = matrix_ref[order_smem[1, place]]
+        modelled = blur(shifted_ref, jnp.maximum(cell, 0) * 4, matrix, joined_ref.at[lane])
+        squares = modelled * modelled
+        squares = squares.reshape(block // 8, 8, LANES).sum(axis=0)
+        sums_ref[row] += jnp.where(cell >= 0, squares, 0.0)
+        hold_turns(modelled.astype(jnp.bfloat16).astype(jnp.float32), turned_ref.at[lane])
+
+    def backward(place, lane):
+        kept = same(place)
+        matrix = matrix_ref[order_smem[1, place]]
+        left, right = blur_back(turned_ref.at[lane], matrix, behind_ref.at[lane])
+        running_ref[place + 1, 0] = left + jnp.where(kept, running_ref[place, 0], 0.0)
+        running_ref[place + 1, 1] = right + jnp.where(kept, running_ref[place, 1], 0.0)
+
+    def normal_pass(row, between):
+        for lane in range(CAP):
+            forward(row, lane, lane)
+
+        @pl.loop(1, slots // CAP)
+        def _(step):
+            for lane in range(CAP):
+                backward(CAP * (step - 1) + lane, lane)
+            for lane in range(CAP):
+                forward(row, CAP * step + lane, lane)
+
+        between()
+        for lane in range(CAP):
+            backward(slots - CAP + lane, lane)
 
     gather_field(0)
     take_edges(0)
     clear_outside(0)
     shift_field(field_ref.at[0], shifted_ref, per_row, sums_ref, 0)
-    normal_pass(1)
+    normal_pass(1, lambda: None)
     gather_field(1)
     take_edges(1)
     clear_outside(1)
     damp(1)
     shift_field(field_ref.at[1], shifted_ref, per_row, sums_ref, 2)
-    normal_pass(3)
-
-    def sum_copies(axis, place, size, source, landed, sems):
-        return [
-            pltpu.make_async_remote_copy(
-                src_ref=source,
-                dst_ref=landed.at[step - 1],
-                send_sem=sems.at[0, step - 1],
-                recv_sem=sems.at[1, step - 1],
-                device_id={axis: lax.rem(place + step, size)},
-                device_id_type=pl.DeviceIdType.MESH,
-            )
-            for step in range(1, size)
-        ]
-
-    rows = lax.broadcasted_iota(jnp.int32, (8, LANES), 0)
-    packed = jnp.zeros((8, LANES), jnp.float32)
-    for number in range(4):
-        packed = jnp.where(rows == number, jnp.sum(sums_ref[number], axis=0, keepdims=True), packed)
-    total_ref[0] = packed
-    ty_copies = sum_copies("ty", ty, ty_size, total_ref.at[0], ty_land_ref, ty_sems)
-    for copy in ty_copies:
-        copy.start()
-    assemble(running_ref, index_smem, per_row, field_ref.at[2])
-    share_edges(2)
-    for copy in ty_copies:
-        copy.wait()
-    partial = total_ref[0]
-    for step in range(ty_size - 1):
-        partial = partial + ty_land_ref[step]
-    total_ref[1] = partial
-    tx_copies = sum_copies("tx", tx, tx_size, total_ref.at[1], tx_land_ref, tx_sems)
-    for copy in tx_copies:
-        copy.start()
+    def sum_copy(step):
+        peer = lax.rem(ty * tx_size + tx + step, ty_size * tx_size)
+        return pltpu.make_async_remote_copy(
+            src_ref=total_ref,
+            dst_ref=total_land_ref.at[step],
+            send_sem=sum_sems.at[0, step],
+            recv_sem=sum_sems.at[1, step],
+            device_id={"ty": peer // tx_size, "tx": lax.rem(peer, tx_size)},
+            device_id_type=pl.DeviceIdType.MESH,
+        )
+
+    def send_sums():
+        packed = jnp.zeros((1, LANES), jnp.float32)
+        for number in range(4):
+            value = jnp.sum(sums_ref[number], axis=0, keepdims=True)
+            value = jnp.sum(value, axis=1, keepdims=True)
+            packed = jnp.where(lanes_of(packed.shape) == number, value, packed)
+        total_ref[...] = packed
+        total_land_ref[0] = packed
+
+        @pl.loop(1, ty_size * tx_size)
+        def _(step):
+            sum_copy(step).start()
+
+    normal_pass(3, send_sums)
+    gather_field(2)
     take_edges(2)
     damp(2)
-    for copy in tx_copies:
-        copy.wait()
-    partial = total_ref[1]
-    for step in range(tx_size - 1):
-        partial = partial + tx_land_ref[step]
-    sums = jnp.broadcast_to(jnp.sum(partial, axis=1, keepdims=True), (8, LANES))
-    r00 = sums[0:1]
-    r01 = sums[1:2] + damping * r00
-    r11 = sums[2:3]
-    r12 = sums[3:4] + damping * r11
+
+    @pl.loop(1, ty_size * tx_size)
+    def _(step):
+        sum_copy(step).wait()
+
+    total = total_land_ref[0]
+    for step in range(1, ty_size * tx_size):
+        total = total + total_land_ref[step]
+    wide = jnp.zeros((1, LANES), jnp.float32)
+    sums = [
+        wide + jnp.sum(jnp.where(lanes_of(wide.shape) == number, total, 0.0), axis=1, keepdims=True)
+        for number in range(4)
+    ]
+    r00 = sums[0]
+    r01 = sums[1] + damping * r00
+    r11 = sums[2]
+    r12 = sums[3] + damping * r11
     step0 = r00 / r01
     norm_next = r00 - 2.0 * step0 * r01 + step0 * step0 * r11
     grown = 1.0 + norm_next / r00
@@ -638,7 +649,7 @@
     smem = pl.BlockSpec(memory_space=pltpu.SMEM)
     dma = pltpu.SemaphoreType.DMA
     scratch = [
-        pltpu.VMEM((frame_count, 48, LANES), f32),
+        pltpu.VMEM((GROUP, frame_count, LANES), f32),
         pltpu.VMEM((frame_count, 16, LANES), bf16),
         pltpu.VMEM((tx_size, CAP, ROWS, LANES), bf16),
         pltpu.VMEM((tx_size, CAP, ROWS, LANES), bf16),
@@ -651,9 +662,9 @@
         pltpu.VMEM((slots, 256, 256), bf16),
         pltpu.VMEM((slots, 2, PATCH, LANES), f32),
         pltpu.VMEM((slots + 1, 2, PATCH, LANES), f32),
-        pltpu.VMEM((4, PAD + ROWS, LANES), f32),
-        pltpu.VMEM((2, 8 + PATCH, LANES), f32),
-        pltpu.VMEM((4, ROWS - 8, LANES), f32),
+        pltpu.VMEM((CAP, 4, PAD + ROWS, LANES), f32),
+        pltpu.VMEM((CAP, 2, 8 + PATCH, LANES), f32),
+        pltpu.VMEM((CAP, 4, ROWS - 8, LANES), f32),
         pltpu.VMEM((4 * per_row * per_row, PATCH, LANES), bf16),
         pltpu.VMEM((3, per_row + 1, tall, LANES), f32),
         pltpu.VMEM((3, 2, per_row + 1, EDGE, LANES), WIRE),
@@ -662,15 +673,13 @@
         pltpu.VMEM((3, 2, EXTENT // 4, LANES), WIRE),
         pltpu.VMEM((3, 2, 2, EDGE, LANES), WIRE),
         pltpu.VMEM((4, 8, LANES), f32),
-        pltpu.VMEM((2, 8, LANES), f32),
-        pltpu.VMEM((ty_size - 1, 8, LANES), f32),
-        pltpu.VMEM((tx_size - 1, 8, LANES), f32),
+        pltpu.VMEM((1, LANES), f32),
+        pltpu.VMEM((ty_size * tx_size, 1, LANES), f32),
         dma((2, tx_size)),
         dma((2, tx_size)),
         dma,
         dma((2, 3, len(SIDES))),
-        dma((2, ty_size - 1)),
-        dma((2, tx_size - 1)),
+        dma((2, ty_size * tx_size)),
     ]
     return pl.pallas_call(
         functools.partial(whole_kernel, (ty_size, tx_size)),
@@ -678,9 +687,11 @@
         in_specs=[vmem, vmem, smem, smem, smem],
         out_specs=(vmem, vmem),
         scratch_shapes=scratch,
-        compiler_params=pltpu.CompilerParams(collective_id=0, has_side_effects=True),
+        compiler_params=pltpu.CompilerParams(
+            collective_id=0, has_side_effects=True, vmem_limit_bytes=36 * 1024 * 1024
+        ),
         name="whole",
-    )(exposures, point_spread, warp_steps, column[:, 0], block_cell)
+    )(exposures, point_spread.transpose(1, 0, 2), warp_steps.T, column[:, 0], block_cell)
 
 
 def solution(mesh):

time: 84.2 us -> 68 us (0.81)
  Pallas kernels: 77.1 us -> 62.6 us
  local copies, waits for them, and re-layouts: 6.25 us -> 4.56 us
    pallas_call x1, Pallas kernels: 77.1 us -> 62.6 us  [body(): pl.pallas_call(functools.partial(whole_kernel, (ty_size, tx_size)), out_s...]
    unnamed x8 -> x12, local copies, waits for them, and re-layouts: 6.25 us -> 4.56 us
where the time goes in v2:
time: 68 us; the launch traced here: 67.8 us
  Pallas kernels  62.6 us (92%)
  local copies, waits for them, and re-layouts  4.56 us (7%)
    pallas_call x1, Pallas kernels, body(): pl.pallas_call(functools.partial(whole_kernel, (ty_size, tx_size)), out_s...  62.6 us
    unnamed x12, local copies, waits for them, and re-layouts  4.56 us

profile of v2, /device:TPU:0, one launch (start us, length us, event | category | flops | bytes accessed | tf_op | source)
XLA Modules:
  0.0 67.8 jit_solution(13969926777653663356)
XLA Ops:
  0.6 0.0 copy-start.4
  0.6 0.0 copy-start.2
  0.7 0.0 copy-start.3
  0.7 0.6 copy-done.4
  1.3 0.0 copy-done.2
  1.3 0.0 copy-done.3
  1.3 0.0 copy-start
  1.3 1.0 %copy-done = f32[8,128,128]{2,1,0:T(8,128)S(1)} copy-done((f32[8,128,128]{2,1,0:T(8,128)S(1)}, f32[8,128,128]{2,1,0:T(8,128)}, u32[]{:S(2)}) %copy-start) | copy-done | bytes 524312
  2.4 0.0 copy-start.1
  2.4 0.9 %copy-done.1 = f32[8,31,31]{2,0,1:T(8,128)S(1)} copy-done((f32[8,31,31]{2,0,1:T(8,128)S(1)}, f32[8,31,31]{2,0,1:T(8,128)}, u32[]{:S(2)}) %copy-start.1) | copy-done | bytes 30776
  3.3 62.6 %whole.1 = (f32[512,512]{1,0:T(8,128)S(1)}, f32[512,512]{1,0:T(8,128)S(1)}) custom-call(f32[8,128,128]{2,1,0:T(8,128)S(1)} %copy-done, f32[31,8,31]{2,1,0:T(8,128)S(1)} %bitcast.3, s32[2,8]{1,0:T(2,128)S(1)} %bitcast.4, s32[8]{0:T(128)S(1)} %bitcast.5, s32[8]{0:T(128)S(1)} %copy-done.4), custom_call_target="tpu_custom_call" | custom-call | tf_op jit(solution)/shard_map/whole/pallas_call | solution.py:684
  65.9 1.0 %copy.9 = f32[512,512]{1,0:T(8,128)} copy(f32[512,512]{1,0:T(8,128)S(1)} %get-tuple-element.4) | data formatting | bytes 2097152
  66.8 1.0 %copy.10 = f32[512,512]{1,0:T(8,128)} copy(f32[512,512]{1,0:T(8,128)S(1)} %get-tuple-element.5) | data formatting | bytes 2097152
Async XLA Ops:
  0.6 0.7 copy-start.4
  0.6 0.7 %copy-start.2 = (s32[8,2]{0,1:T(2,128)S(1)}, s32[8,2]{0,1:T(2,128)}, u32[]{:S(2)}) copy-start(s32[8,2]{0,1:T(2,128)} %param.7) | copy-start | bytes 196
  0.7 0.7 %copy-start.3 = (s32[8,1]{0,1:T(1,128)S(1)}, s32[8,1]{0,1:T(1,128)}, u32[]{:S(2)}) copy-start(s32[8,1]{0,1:T(1,128)} %param.8) | copy-start | bytes 100
  1.3 1.0 %copy-start = (f32[8,128,128]{2,1,0:T(8,128)S(1)}, f32[8,128,128]{2,1,0:T(8,128)}, u32[]{:S(2)}) copy-start(f32[8,128,128]{2,1,0:T(8,128)} %exposures_ref.1) | copy-start | bytes 1572868
  2.4 0.9 %copy-start.1 = (f32[8,31,31]{2,0,1:T(8,128)S(1)}, f32[8,31,31]{2,0,1:T(8,128)}, u32[]{:S(2)}) copy-start(f32[8,31,31]{2,0,1:T(8,128)} %param.6) | copy-start | bytes 92260

commit v3 on v2

--- a/solution.py
+++ b/solution.py
@@ -164,15 +164,14 @@
 
 
 def shift_field(field_ref, shifted_ref, per_row, sums_ref, row):
-    chunk = 16
+    chunk = PATCH // 2
 
     tall = PATCH // chunk
 
     @pl.loop(0, per_row * tall)
     def _(step):
-        number = step // tall * (LANES // chunk) + lax.rem(step, tall)
-        start = pl.multiple_of(number * chunk, chunk)
-        local = pl.multiple_of(lax.rem(step, tall) * chunk, chunk)
+        local = pl.multiple_of(lax.rem(step, tall) * chunk, 16)
+        start = pl.multiple_of(step // tall * LANES + local, 16)
         cell = step // tall * per_row
         lanes = lanes_of((chunk, LANES))
         low, middle = lanes < 64, (lanes >= 32) & (lanes < 96)
@@ -199,11 +198,11 @@
             if col == per_row:
                 value = jnp.where(lanes < MARGIN, value, 0.0)
             squares = value * value if squares is None else squares + value * value
-        once = (lax.rem(step, tall) < LANES // chunk) | (cell == per_row * (per_row - 1))
-        place = start + lax.broadcasted_iota(jnp.int32, squares.shape, 0)
-        squares = jnp.where((place >= MARGIN) & (place < EXTENT - MARGIN), squares, 0.0)
-        squares = squares.reshape(chunk // 8, 8, LANES).sum(axis=0)
-        sums_ref[row] += jnp.where(once, squares, 0.0)
+        place = lax.broadcasted_iota(jnp.int32, squares.shape, 0)
+        last = jnp.where(cell == per_row * (per_row - 1), LANES, 0)
+        inside = (place + start >= MARGIN) & (place + start < EXTENT - MARGIN)
+        squares = jnp.where(inside & (place + local < LANES + last), squares, 0.0)
+        sums_ref[row] += squares.reshape(chunk // 8, 8, LANES).sum(axis=0)
 
 
 def whole_kernel(
@@ -332,12 +331,12 @@
 
     tags_ref[0] = tags_for(0)
 
-    @pl.loop(1, tx_size)
+    @pl.loop(1, tx_size, unroll=True)
     def _(step):
         tag_send_ref[step] = tags_for(step)
         tag_copy(step).start()
 
-    @pl.loop(1, tx_size)
+    @pl.loop(1, tx_size, unroll=True)
     def _(step):
         fill(send_ref, step)
         frame_copy(step).start()
@@ -356,7 +355,7 @@
 
     first_pass(0)
 
-    @pl.loop(1, tx_size)
+    @pl.loop(1, tx_size, unroll=True)
     def _(step):
         tag_copy(step).wait()
 
@@ -403,7 +402,7 @@
         before = order_smem[2, jnp.maximum(place - 1, 0)]
         return (place > 0) & (before == order_smem[2, place])
 
-    @pl.loop(0, slots)
+    @pl.loop(0, slots, unroll=4)
     def _(place):
         kept = same(place)
         slot = order_smem[1, place]
@@ -620,7 +619,7 @@
     y1 = -step0 - step1 * grown
     y2 = step1 * step0
 
-    chunk = 32
+    chunk = 128
 
     @pl.loop(0, TILE // chunk)
     def _(number):

time: 68 us -> 62.1 us (0.913)
  Pallas kernels: 62.6 us -> 56.6 us
    pallas_call x1, Pallas kernels: 62.6 us -> 56.6 us  [body(): pl.pallas_call(functools.partial(whole_kernel, (ty_size, tx_size)), out_s...]
where the time goes in v3:
time: 62.1 us; the launch traced here: 61.9 us
  Pallas kernels  56.6 us (91%)
  local copies, waits for them, and re-layouts  4.56 us (7%)
  between operations  0.67 us (1%)
    pallas_call x1, Pallas kernels, body(): pl.pallas_call(functools.partial(whole_kernel, (ty_size, tx_size)), out_s...  56.6 us
    unnamed x12, local copies, waits for them, and re-layouts  4.56 us

profile of v3, /device:TPU:0, one launch (start us, length us, event | category | flops | bytes accessed | tf_op | source)
XLA Modules:
  0.0 61.9 jit_solution(2352439457000489930)
XLA Ops:
  0.6 0.0 copy-start.4
  0.6 0.0 copy-start.2
  0.7 0.0 copy-start.3
  0.7 0.6 %copy-done.4 = s32[8]{0:T(128)S(1)} copy-done((s32[8]{0:T(128)S(1)}, s32[8]{0:T(128)}, u32[]{:S(2)}) %copy-start.4) | copy-done | bytes 56
  1.3 0.0 copy-done.2
  1.3 0.0 copy-done.3
  1.3 0.0 copy-start
  1.3 1.0 %copy-done = f32[8,128,128]{2,1,0:T(8,128)S(1)} copy-done((f32[8,128,128]{2,1,0:T(8,128)S(1)}, f32[8,128,128]{2,1,0:T(8,128)}, u32[]{:S(2)}) %copy-start) | copy-done | bytes 524312
  2.4 0.0 copy-start.1
  2.4 0.9 %copy-done.1 = f32[8,31,31]{2,0,1:T(8,128)S(1)} copy-done((f32[8,31,31]{2,0,1:T(8,128)S(1)}, f32[8,31,31]{2,0,1:T(8,128)}, u32[]{:S(2)}) %copy-start.1) | copy-done | bytes 30776
  3.3 56.6 %whole.1 = (f32[512,512]{1,0:T(8,128)S(1)}, f32[512,512]{1,0:T(8,128)S(1)}) custom-call(f32[8,128,128]{2,1,0:T(8,128)S(1)} %copy-done, f32[31,8,31]{2,1,0:T(8,128)S(1)} %bitcast.3, s32[2,8]{1,0:T(2,128)S(1)} %bitcast.4, s32[8]{0:T(128)S(1)} %bitcast.5, s32[8]{0:T(128)S(1)} %copy-done.4), custom_call_target="tpu_custom_call" | custom-call | tf_op jit(solution)/shard_map/whole/pallas_call | solution.py:683
  59.9 1.0 %copy.9 = f32[512,512]{1,0:T(8,128)} copy(f32[512,512]{1,0:T(8,128)S(1)} %get-tuple-element.4) | data formatting | bytes 2097152
  60.9 1.0 %copy.10 = f32[512,512]{1,0:T(8,128)} copy(f32[512,512]{1,0:T(8,128)S(1)} %get-tuple-element.5) | data formatting | bytes 2097152
Async XLA Ops:
  0.6 0.7 %copy-start.4 = (s32[8]{0:T(128)S(1)}, s32[8]{0:T(128)}, u32[]{:S(2)}) copy-start(s32[8]{0:T(128)} %cell_ref.1) | copy-start | bytes 100
  0.6 0.7 %copy-start.2 = (s32[8,2]{0,1:T(2,128)S(1)}, s32[8,2]{0,1:T(2,128)}, u32[]{:S(2)}) copy-start(s32[8,2]{0,1:T(2,128)} %param.7) | copy-start | bytes 196
  0.7 0.7 %copy-start.3 = (s32[8,1]{0,1:T(1,128)S(1)}, s32[8,1]{0,1:T(1,128)}, u32[]{:S(2)}) copy-start(s32[8,1]{0,1:T(1,128)} %param.8) | copy-start | bytes 100
  1.3 1.0 %copy-start = (f32[8,128,128]{2,1,0:T(8,128)S(1)}, f32[8,128,128]{2,1,0:T(8,128)}, u32[]{:S(2)}) copy-start(f32[8,128,128]{2,1,0:T(8,128)} %exposures_ref.1) | copy-start | bytes 1572868
  2.4 0.9 %copy-start.1 = (f32[8,31,31]{2,0,1:T(8,128)S(1)}, f32[8,31,31]{2,0,1:T(8,128)}, u32[]{:S(2)}) copy-start(f32[8,31,31]{2,0,1:T(8,128)} %param.6) | copy-start | bytes 92260
